TPU v7x, 512 devices: a whole 4x4x16 slice. The times are simulated.
512 devices in a mesh: dp: 64 (over z_lo, x, core), ens: 8 (over y, z_hi).
Axes of the slice: x: 4, y: 4, z: 16 (z_hi: 2, z_lo: 8; z = z_hi * 8 + z_lo), core: 2. Of those that a mesh axis runs over, the one named last changes fastest.
Arguments:
- embeddings: bfloat16 [49152, 1024], P('dp'), may hold values from -6 to 6
- valid_mask: int32 [49152], P('dp'), may hold values 0 or 1
- first_weight: bfloat16 [8, 1024, 4096], P(None, 'dp', 'ens'), may hold values from -0.1875 to 0.1875
- second_weight: bfloat16 [8, 4096, 128], P(None, 'ens'), may hold values from -0.09375 to 0.09375
- thresholds: int32 [8], replicated, may hold values from -256 to 256
Outputs:
- mean_logits: float32 [49152, 128], P('dp')
- kept_share: float32 [8], P('ens')
- agree_share: float32 [8], P('ens')
All inputs are finite; a program needn't handle non-finite values. No bound on the sum of `valid_mask` on one device may be relied on, other than what follows from the above.
Results may differ from a plain program's by a relative error of at most 0.0044.
Values may be sent and summed in bfloat16 or wider, within the bound.
A program may use at most 64 MiB of HBM per device.

v0:
```python
import jax
import jax.numpy as jnp
from jax import lax
from jax.sharding import PartitionSpec as P


def split_up(shard, dim, size):
    shape = shard.shape
    blocks = shard.reshape(*shape[:dim], size, shape[dim] // size, *shape[dim + 1 :])
    return jnp.moveaxis(blocks, dim, 0)


def cut_rows(length, count):
    lap = length // count
    if lap >= 8:
        lap -= lap % 8
    return [lap * k for k in range(1, count)]


def in_order(blocks, dim):
    shape = list(blocks.shape[1:])
    shape[dim] *= blocks.shape[0]
    return jnp.moveaxis(blocks, 0, dim).reshape(shape)


def several_exchanges(shard, axis, pieces, split_dim, concat_dim):
    blocks = split_up(shard, split_dim, lax.axis_size(axis))
    split_at = max(range(1, max(2, blocks.ndim - 1)), key=lambda d: blocks.shape[d])
    done = []
    for section in jnp.split(blocks, cut_rows(blocks.shape[split_at], pieces), axis=split_at):
        if section.size:
            done.append(lax.all_to_all(section, axis, split_axis=0, concat_axis=0, tiled=True))
    return in_order(jnp.concatenate(done, axis=split_at), concat_dim)


def from_everyone(shard, axis):
    copies = jnp.broadcast_to(shard, (lax.axis_size(axis), *shard.shape))
    return lax.all_to_all(copies, axis, split_axis=0, concat_axis=0, tiled=True)


def over_copies(shard, axis):
    everything = from_everyone(shard, axis)
    return jnp.sum(everything.astype(jnp.float32), axis=0)


def of_everyone(shard, axis):
    return from_everyone(shard, axis).sum(axis=0)


def in_one(arrays, axis):
    ends = [0]
    for a in arrays:
        ends.append(ends[-1] + a.size)
    total = of_everyone(jnp.concatenate([a.ravel() for a in arrays]), axis)
    return tuple((total[b:e].reshape(a.shape) for a, b, e in zip(arrays, ends, ends[1:])))


def on_device(embeddings, valid_mask, first_weight, second_weight, thresholds):
    member = lax.axis_index("ens")
    own_first = lax.all_to_all(first_weight, "ens", split_axis=0, concat_axis=2, tiled=True)
    own_second = several_exchanges(second_weight, "ens", 2, 0, 1)
    full_first = lax.all_gather(own_first[0], "dp", axis=0, tiled=True)
    hidden = jnp.maximum(
        jnp.dot(embeddings, full_first, preferred_element_type=jnp.float32), 0.0
    ).astype(jnp.bfloat16)
    logits_own = jnp.dot(hidden, own_second[0], preferred_element_type=jnp.float32)
    classes = logits_own.shape[1]
    levels = jnp.arange(classes, dtype=jnp.float32)
    grades = (2.0 * levels / (classes - 1) - 1.0) * jnp.sqrt(jnp.float32(3.0 / classes))
    scores = jnp.dot(logits_own, grades, precision=lax.Precision.HIGHEST)
    cutoffs = thresholds.astype(jnp.float32) / 256.0
    own_cutoff = lax.dynamic_index_in_dim(cutoffs, member, 0, keepdims=False)
    validity = valid_mask.astype(jnp.float32)
    kept_soft = validity * jax.nn.sigmoid(4.0 * (scores - own_cutoff))
    mean_logits = (
        over_copies(logits_own.astype(jnp.bfloat16), "ens").astype(jnp.float32)
        / first_weight.shape[0]
    )
    ens_score = jnp.dot(mean_logits, grades, precision=lax.Precision.HIGHEST)
    ens_kept = jax.nn.sigmoid(4.0 * (ens_score - jnp.mean(cutoffs)))
    agree_local = jnp.sum(kept_soft * ens_kept)
    kept_total, agree_total = in_one((jnp.sum(kept_soft), agree_local), "dp")
    shard_docs = embeddings.shape[0]
    return (
        mean_logits,
        (kept_total / shard_docs).reshape(1),
        (agree_total / shard_docs).reshape(1),
    )


def solution(mesh):
    return jax.shard_map(
        on_device,
        mesh=mesh,
        in_specs=(P("dp", None), P("dp"), P(None, "dp", "ens"), P(None, "ens", None), P()),
        out_specs=(P("dp", None), P("ens"), P("ens")),
        check_vma=False,
    )
```

profile of v0, /device:TPU:1, one launch (start us, length us, event | category | flops | bytes accessed | tf_op | source)
XLA Modules:
  0.0 333.6 jit_solution(111445874965293776)
XLA Ops:
  7.2 0.0 copy-start
  7.2 0.0 all-gather.2.cloned.1.call-start
  7.2 32.7 %all_to_all.36 = bf16[8,16,512]{2,1,0:T(8,128)(2,1)S(1)} all-to-all(bf16[8,16,512]{2,1,0:T(8,128)(2,1)} %param.7), channel_id=1, replica_groups=mesh['dp'=64,'ens'=8] {'ens'}, dimensions={0} | all-to-all | bytes 262144 | tf_op jit(solution)/shard_map/all_to_all | solution.py:60
  39.9 0.7 copy.16
  40.5 0.0 all-gather.2.cloned.1.call-update
  40.6 1.3 fusion.12
  41.9 19.8 %all_to_all.37 = bf16[8,1,256,128]{3,2,1,0:T(8,128)(2,1)S(1)} all-to-all(bf16[8,1,256,128]{3,2,1,0:T(8,128)(2,1)S(1)} %get-tuple-element.6), channel_id=1, replica_groups=mesh['dp'=64,'ens'=8] {'ens'}, dimensions={0} | all-to-all | bytes 1048576 | tf_op jit(solution)/shard_map/all_to_all | solution.py:32
  61.7 27.5 %all_to_all.38 = bf16[8,1,256,128]{3,2,1,0:T(8,128)(2,1)S(1)} all-to-all(bf16[8,1,256,128]{3,2,1,0:T(8,128)(2,1)S(1)} %get-tuple-element.5), channel_id=1, replica_groups=mesh['dp'=64,'ens'=8] {'ens'}, dimensions={0} | all-to-all | bytes 1048576 | tf_op jit(solution)/shard_map/all_to_all | solution.py:32
  89.2 0.1 pad_maximum_fusion
  89.3 104.5 %all-gather.2.cloned.1.call-done = bf16[1024,4096]{1,0:T(8,128)(2,1)} async-done(((bf16[16,4096]{1,0:T(8,128)(2,1)}), bf16[1024,4096]{1,0:T(8,128)(2,1)}) %all-gather.2.cloned.1.call-update) | async-done | bytes 8388624 | tf_op jit(solution)/shard_map/all_gather | solution.py:62
  193.7 0.0 copy-done
  193.8 11.8 %fusion.14 = (bf16[768,128]{1,0:T(8,128)(2,1)S(1)}, f32[768,128]{1,0:T(8,128)S(1)}) fusion(bf16[4096,128]{1,0:T(8,128)(2,1)S(1)} %bitcast.25, bf16[768,1024]{1,0:T(8,128)(2,1)S(1)} %copy-done, bf16[1024,4096]{1,0:T(8,128)(2,1)} %all-gather.2.cloned.1.call-done), kind=kOutput, calls=%fused_computation.25 | convolution fusion | flops 7254147072 | bytes 11599872 | tf_op jit(solution)/shard_map/dot_general | solution.py:66
  205.5 0.0 copy-start.3
  205.6 1.4 broadcast_in_dim.6
  206.9 0.0 copy-start.2
  206.9 11.8 %all-to-all-start.3 = ((bf16[8,768,128]{2,1,0:T(8,128)(2,1)}), bf16[8,768,128]{2,1,0:T(8,128)(2,1)S(1)}, u32[]{:S(2)}, u32[]{:S(2)}) async-start(bf16[8,768,128]{2,1,0:T(8,128)(2,1)} %broadcast_in_dim.6), calls=%async_computation.3 | async-start | bytes 3145728 | tf_op jit(solution)/shard_map/all_to_all | solution.py:38
  218.7 0.0 copy-done.3
  218.7 0.6 fusion.10
  219.3 0.6 dynamic_slice.4
  220.5 0.5 convolution_reduce_fusion.1
  221.0 34.4 %all-to-all-done.3 = bf16[8,768,128]{2,1,0:T(8,128)(2,1)S(1)} async-done(((bf16[8,768,128]{2,1,0:T(8,128)(2,1)}), bf16[8,768,128]{2,1,0:T(8,128)(2,1)S(1)}, u32[]{:S(2)}, u32[]{:S(2)}) %all-to-all-start.3) | async-done | bytes 1572896 | tf_op jit(solution)/shard_map/all_to_all | solution.py:38
  255.4 0.2 convert_reduce_fusion
  255.7 0.0 copy-start.1
  255.7 0.5 convolution_reduce_fusion
  256.1 0.0 copy-done.2
  256.1 1.3 fusion.11
  257.5 1.4 pad_maximum_fusion.1
  258.9 63.6 %all_to_all.39 = f32[64,1,2]{2,1,0:T(1,128)S(1)} all-to-all(f32[64,1,2]{2,1,0:T(1,128)S(1)} %broadcast_in_dim.7), channel_id=1, replica_groups=mesh['dp'=64,'ens'=8] {'dp'}, dimensions={0} | all-to-all | bytes 1024 | tf_op jit(solution)/shard_map/all_to_all | solution.py:38
  322.5 0.1 reduce_sum.49
  322.6 0.6 fusion.13
  324.5 0.0 copy-done.1
  (2 shorter events, 0.1 us)
Async XLA Ops:
  7.2 186.6 %copy-start = (bf16[768,1024]{1,0:T(8,128)(2,1)S(1)}, bf16[768,1024]{1,0:T(8,128)(2,1)}, u32[]{:S(2)}) copy-start(bf16[768,1024]{1,0:T(8,128)(2,1)} %param.5) | copy-start | bytes 4718596
  7.2 186.6 %all-gather.2.cloned.1.call-start = ((), (), s32[]{:S(2)}) async-start(), calls=%async_computation.5 | async-start | bytes 8519680 | tf_op jit(solution)/shard_map/all_gather | solution.py:62
  205.5 13.1 %copy-start.3 = (s32[8]{0:T(128)S(1)}, s32[8]{0:T(128)}, u32[]{:S(2)}) copy-start(s32[8]{0:T(128)} %param.9) | copy-start | bytes 100
  206.9 49.2 %copy-start.2 = (s32[768]{0:T(1024)S(1)}, s32[768]{0:T(1024)}, u32[]{:S(2)}) copy-start(s32[768]{0:T(1024)} %param.6) | copy-start | bytes 9220
  206.9 48.5 %all-to-all-start.3 = ((bf16[8,768,128]{2,1,0:T(8,128)(2,1)}), bf16[8,768,128]{2,1,0:T(8,128)(2,1)S(1)}, u32[]{:S(2)}, u32[]{:S(2)}) async-start(bf16[8,768,128]{2,1,0:T(8,128)(2,1)} %broadcast_in_dim.6), calls=%async_computation.3 | async-start | bytes 3145728 | tf_op jit(solution)/shard_map/all_to_all | solution.py:38
  255.7 68.9 %copy-start.1 = (f32[768,128]{1,0:T(8,128)}, f32[768,128]{1,0:T(8,128)S(1)}, u32[]{:S(2)}) copy-start(f32[768,128]{1,0:T(8,128)S(1)} %broadcast_multiply_fusion) | copy-start | bytes 1179652
Sparse Core Ops, SparseCore 0:
  40.7 153.0 all-gather.1
where the time goes:
time: 334 us
  blocking collectives  144 us (43%)
  waiting for transfers between devices  139 us (42%)
  between operations  18.3 us (5%)
  matrix products  12.7 us (4%)
  starting transfers between devices  11.8 us (4%)
  local copies, waits for them, and re-layouts  4.51 us (1%)
  other arithmetic  3.76 us (1%)
    all_gather x1, waiting for transfers between devices, on_device(): full_first = lax.all_gather(own_first[0], 'dp', axis=0, tiled=True)  104 us
    all_to_all x1, blocking collectives, from_everyone(): return lax.all_to_all(copies, axis, split_axis=0, concat_axis=0, tiled=True)  63.6 us
    all_to_all x2, blocking collectives, several_exchanges(): lax.all_to_all(section, axis, split_axis=0, concat_axis=0, tiled=True)  47.4 us
    all_to_all x1, waiting for transfers between devices, from_everyone(): return lax.all_to_all(copies, axis, split_axis=0, concat_axis=0, tiled=True)  34.4 us
    all_to_all x1, blocking collectives, on_device(): lax.all_to_all(first_weight, 'ens', split_axis=0, concat_axis=2, tiled=True)  32.7 us
    dot_general x1, matrix products, on_device(): jnp.dot(hidden, own_second[0], preferred_element_type=jnp.float32)  11.8 us
    all_to_all x1, starting transfers between devices, from_everyone(): return lax.all_to_all(copies, axis, split_axis=0, concat_axis=0, tiled=True)  11.8 us
  transfers between devices with their start and end apart: 2, of which 2 were waited for; matrix products, arithmetic and copies ran while one was open for 1% of the time, Pallas kernels for 0%

commit v1 on v0

--- a/solution.py
+++ b/solution.py
@@ -59,7 +59,13 @@
     member = lax.axis_index("ens")
     own_first = lax.all_to_all(first_weight, "ens", split_axis=0, concat_axis=2, tiled=True)
     own_second = several_exchanges(second_weight, "ens", 2, 0, 1)
-    full_first = lax.all_gather(own_first[0], "dp", axis=0, tiled=True)
+    field_in = own_first[0]
+    full_first = jnp.concatenate(
+        lax.all_to_all(
+            jnp.stack([field_in] * lax.psum(1, "dp")), "dp", split_axis=0, concat_axis=0
+        ),
+        axis=0,
+    )
     hidden = jnp.maximum(
         jnp.dot(embeddings, full_first, preferred_element_type=jnp.float32), 0.0
     ).astype(jnp.bfloat16)

time: 334 us -> 603 us (1.81)
  waiting for transfers between devices: 139 us -> 439 us
  blocking collectives: 144 us -> 68.1 us
  starting transfers between devices: 11.8 us -> 63.3 us
  between operations: 18.3 us -> 4.95 us
    all_to_all x0 -> x3, waiting for transfers between devices: none -> 393 us  [the longest x1 365 us: on_device(): lax.all_to_all(jnp.stack([field_in] * lax.psum(1, 'dp')), 'dp', split_axi...]
    all_gather x1 -> x0, waiting for transfers between devices: 104 us -> none  [on_device(): full_first = lax.all_gather(own_first[0], 'dp', axis=0, tiled=True)]
    all_to_all x0 -> x3, starting transfers between devices: none -> 54.6 us  [the longest x1 32.7 us: on_device(): lax.all_to_all(jnp.stack([field_in] * lax.psum(1, 'dp')), 'dp', split_axi...]
    all_to_all x1 -> x0, blocking collectives: 32.7 us -> none  [on_device(): lax.all_to_all(first_weight, 'ens', split_axis=0, concat_axis=2, tiled=True)]
    all_to_all x2 -> x1, blocking collectives: 47.4 us -> 19.8 us  [several_exchanges(): lax.all_to_all(section, axis, split_axis=0, concat_axis=0, tiled=True)]
    all_to_all x1, blocking collectives: 63.6 us -> 48.3 us  [from_everyone(): return lax.all_to_all(copies, axis, split_axis=0, concat_axis=0, tiled=True)]
    all_to_all x1, waiting for transfers between devices: 34.4 us -> 46.3 us  [from_everyone(): return lax.all_to_all(copies, axis, split_axis=0, concat_axis=0, tiled=True)]
  transfers between devices with their start and end apart: 2 -> 4, of which waited for: 2 -> 4; matrix products, arithmetic and copies ran while one was open for 1% -> 1% of each run, Pallas kernels for 0% -> 0%
where the time goes in v1:
time: 603 us; the launch traced here: 602 us
  waiting for transfers between devices  439 us (73%)
  blocking collectives  68.1 us (11%)
  starting transfers between devices  63.3 us (10%)
  matrix products  12.9 us (2%)
  local copies, waits for them, and re-layouts  8.92 us (1%)
    all_to_all x1, waiting for transfers between devices, on_device(): lax.all_to_all(jnp.stack([field_in] * lax.psum(1, 'dp')), 'dp', split_axi...  365 us
    all_to_all x1, blocking collectives, from_everyone(): return lax.all_to_all(copies, axis, split_axis=0, concat_axis=0, tiled=True)  48.3 us
    all_to_all x1, waiting for transfers between devices, from_everyone(): return lax.all_to_all(copies, axis, split_axis=0, concat_axis=0, tiled=True)  46.3 us
    all_to_all x1, starting transfers between devices, on_device(): lax.all_to_all(jnp.stack([field_in] * lax.psum(1, 'dp')), 'dp', split_axi...  32.7 us
    all_to_all x1, blocking collectives, several_exchanges(): lax.all_to_all(section, axis, split_axis=0, concat_axis=0, tiled=True)  19.8 us
    all_to_all x1, starting transfers between devices, on_device(): lax.all_to_all(first_weight, 'ens', split_axis=0, concat_axis=2, tiled=True)  18.4 us
    all_to_all x1, waiting for transfers between devices, several_exchanges(): lax.all_to_all(section, axis, split_axis=0, concat_axis=0, tiled=True)  16.2 us
    all_to_all x1, waiting for transfers between devices, on_device(): lax.all_to_all(first_weight, 'ens', split_axis=0, concat_axis=2, tiled=True)  12.2 us
  transfers between devices with their start and end apart: 4, of which 4 were waited for; matrix products, arithmetic and copies ran while one was open for 1% of the time, Pallas kernels for 0%

profile of v1, /device:TPU:1, one launch (start us, length us, event | category | flops | bytes accessed | tf_op | source)
XLA Modules:
  0.0 602.1 jit_solution(1657625365680144362)
XLA Ops:
  0.6 0.0 copy-start
  0.6 18.4 %all-to-all-start = ((bf16[8,16,512]{2,1,0:T(8,128)(2,1)}), bf16[8,16,512]{2,1,0:T(8,128)(2,1)S(1)}, u32[]{:S(2)}, u32[]{:S(2)}) async-start(bf16[8,16,512]{2,1,0:T(8,128)(2,1)} %param.7), calls=%async_computation | async-start | bytes 262144 | tf_op jit(solution)/shard_map/all_to_all | solution.py:60
  19.0 2.1 fusion.12
  21.1 12.2 %all-to-all-done = bf16[8,16,512]{2,1,0:T(8,128)(2,1)S(1)} async-done(((bf16[8,16,512]{2,1,0:T(8,128)(2,1)}), bf16[8,16,512]{2,1,0:T(8,128)(2,1)S(1)}, u32[]{:S(2)}, u32[]{:S(2)}) %all-to-all-start) | async-done | bytes 131104 | tf_op jit(solution)/shard_map/all_to_all | solution.py:60
  33.3 19.8 %all_to_all.44 = bf16[8,1,256,128]{3,2,1,0:T(8,128)(2,1)S(1)} all-to-all(bf16[8,1,256,128]{3,2,1,0:T(8,128)(2,1)S(1)} %get-tuple-element.6), channel_id=1, replica_groups=mesh['dp'=64,'ens'=8] {'ens'}, dimensions={0} | all-to-all | bytes 1048576 | tf_op jit(solution)/shard_map/all_to_all | solution.py:32
  53.1 3.5 all-to-all-start.2
  56.6 16.2 %all-to-all-done.2 = bf16[8,1,256,128]{3,2,1,0:T(8,128)(2,1)S(1)} async-done(((bf16[8,1,256,128]{3,2,1,0:T(8,128)(2,1)}), bf16[8,1,256,128]{3,2,1,0:T(8,128)(2,1)S(1)}, u32[]{:S(2)}, u32[]{:S(2)}) %all-to-all-start.2) | async-done | bytes 524320 | tf_op jit(solution)/shard_map/all_to_all | solution.py:32
  72.8 4.3 stack.3
  77.1 32.7 %all-to-all-start.1 = ((bf16[64,16,4096]{2,1,0:T(8,128)(2,1)}), bf16[64,16,4096]{2,1,0:T(8,128)(2,1)}, u32[]{:S(2)}, u32[]{:S(2)}) async-start(bf16[64,16,4096]{2,1,0:T(8,128)(2,1)} %stack.3), calls=%async_computation.1 | async-start | bytes 16777216 | tf_op jit(solution)/shard_map/all_to_all | solution.py:64
  109.7 1.1 pad_maximum_fusion
  110.8 364.6 %all-to-all-done.1 = bf16[64,16,4096]{2,1,0:T(8,128)(2,1)} async-done(((bf16[64,16,4096]{2,1,0:T(8,128)(2,1)}), bf16[64,16,4096]{2,1,0:T(8,128)(2,1)}, u32[]{:S(2)}, u32[]{:S(2)}) %all-to-all-start.1) | async-done | bytes 8388640 | tf_op jit(solution)/shard_map/all_to_all | solution.py:64
  475.4 0.0 copy-done
  475.4 12.0 %fusion.14 = (bf16[768,128]{1,0:T(8,128)(2,1)S(1)}, f32[768,128]{1,0:T(8,128)S(1)}) fusion(bf16[4096,128]{1,0:T(8,128)(2,1)} %bitcast.26, bf16[768,1024]{1,0:T(8,128)(2,1)S(1)} %copy-done, bf16[1024,4096]{1,0:T(8,128)(2,1)} %bitcast.2), kind=kOutput, calls=%fused_computation.25 | convolution fusion | flops 7254147072 | bytes 11599872 | tf_op jit(solution)/shard_map/dot_general | solution.py:72
  487.4 0.0 copy-start.3
  487.4 1.4 broadcast_in_dim.6
  488.8 0.0 copy-start.2
  488.8 8.7 %all-to-all-start.4 = ((bf16[8,768,128]{2,1,0:T(8,128)(2,1)}), bf16[8,768,128]{2,1,0:T(8,128)(2,1)S(1)}, u32[]{:S(2)}, u32[]{:S(2)}) async-start(bf16[8,768,128]{2,1,0:T(8,128)(2,1)} %broadcast_in_dim.6), calls=%async_computation.4 | async-start | bytes 3145728 | tf_op jit(solution)/shard_map/all_to_all | solution.py:38
  497.5 0.0 copy-done.3
  497.5 0.6 fusion.10
  498.1 0.6 dynamic_slice.4
  499.4 0.5 convolution_reduce_fusion.1
  499.8 46.3 %all-to-all-done.4 = bf16[8,768,128]{2,1,0:T(8,128)(2,1)S(1)} async-done(((bf16[8,768,128]{2,1,0:T(8,128)(2,1)}), bf16[8,768,128]{2,1,0:T(8,128)(2,1)S(1)}, u32[]{:S(2)}, u32[]{:S(2)}) %all-to-all-start.4) | async-done | bytes 1572896 | tf_op jit(solution)/shard_map/all_to_all | solution.py:38
  546.1 0.2 convert_reduce_fusion
  546.4 0.0 copy-start.1
  546.4 0.5 convolution_reduce_fusion
  546.8 0.0 copy-done.2
  546.9 1.3 fusion.11
  548.2 1.4 pad_maximum_fusion.1
  549.6 48.3 %all_to_all.45 = f32[64,1,2]{2,1,0:T(1,128)S(1)} all-to-all(f32[64,1,2]{2,1,0:T(1,128)S(1)} %broadcast_in_dim.7), channel_id=1, replica_groups=mesh['dp'=64,'ens'=8] {'dp'}, dimensions={0} | all-to-all | bytes 1024 | tf_op jit(solution)/shard_map/all_to_all | solution.py:38
  597.9 0.1 reduce_sum.49
  598.0 0.6 fusion.13
  599.9 0.0 copy-done.1
  (3 shorter events, 0.1 us)
Async XLA Ops:
  0.6 474.8 %copy-start = (bf16[768,1024]{1,0:T(8,128)(2,1)S(1)}, bf16[768,1024]{1,0:T(8,128)(2,1)}, u32[]{:S(2)}) copy-start(bf16[768,1024]{1,0:T(8,128)(2,1)} %param.5) | copy-start | bytes 4718596
  0.6 32.7 %all-to-all-start = ((bf16[8,16,512]{2,1,0:T(8,128)(2,1)}), bf16[8,16,512]{2,1,0:T(8,128)(2,1)S(1)}, u32[]{:S(2)}, u32[]{:S(2)}) async-start(bf16[8,16,512]{2,1,0:T(8,128)(2,1)} %param.7), calls=%async_computation | async-start | bytes 262144 | tf_op jit(solution)/shard_map/all_to_all | solution.py:60
  53.1 19.7 %all-to-all-start.2 = ((bf16[8,1,256,128]{3,2,1,0:T(8,128)(2,1)}), bf16[8,1,256,128]{3,2,1,0:T(8,128)(2,1)S(1)}, u32[]{:S(2)}, u32[]{:S(2)}) async-start(bf16[8,1,256,128]{3,2,1,0:T(8,128)(2,1)} %get-tuple-element.5), calls=%async_computation.2 | async-start | bytes 1048576 | tf_op jit(solution)/shard_map/all_to_all | solution.py:32
  77.1 398.3 %all-to-all-start.1 = ((bf16[64,16,4096]{2,1,0:T(8,128)(2,1)}), bf16[64,16,4096]{2,1,0:T(8,128)(2,1)}, u32[]{:S(2)}, u32[]{:S(2)}) async-start(bf16[64,16,4096]{2,1,0:T(8,128)(2,1)} %stack.3), calls=%async_computation.1 | async-start | bytes 16777216 | tf_op jit(solution)/shard_map/all_to_all | solution.py:64
  487.4 10.1 %copy-start.3 = (s32[8]{0:T(128)S(1)}, s32[8]{0:T(128)}, u32[]{:S(2)}) copy-start(s32[8]{0:T(128)} %param.9) | copy-start | bytes 100
  488.8 58.1 %copy-start.2 = (s32[768]{0:T(1024)S(1)}, s32[768]{0:T(1024)}, u32[]{:S(2)}) copy-start(s32[768]{0:T(1024)} %param.6) | copy-start | bytes 9220
  488.8 57.3 %all-to-all-start.4 = ((bf16[8,768,128]{2,1,0:T(8,128)(2,1)}), bf16[8,768,128]{2,1,0:T(8,128)(2,1)S(1)}, u32[]{:S(2)}, u32[]{:S(2)}) async-start(bf16[8,768,128]{2,1,0:T(8,128)(2,1)} %broadcast_in_dim.6), calls=%async_computation.4 | async-start | bytes 3145728 | tf_op jit(solution)/shard_map/all_to_all | solution.py:38
  546.4 53.5 %copy-start.1 = (f32[768,128]{1,0:T(8,128)}, f32[768,128]{1,0:T(8,128)S(1)}, u32[]{:S(2)}) copy-start(f32[768,128]{1,0:T(8,128)S(1)} %broadcast_multiply_fusion) | copy-start | bytes 1179652
